TPU v7x, 512 devices: a whole 4x8x8 slice. The times are simulated.
512 devices in a mesh: row: 32 (over y, x), col: 16 (over z, core).
Axes of the slice: x: 4, y: 8, z: 8, core: 2. Of those that a mesh axis runs over, the one named last changes fastest.
Arguments:
- pair_factors: float32 [12288, 1024], P(('row', 'col')), may hold values from -0.09375 to 0.09375
- k_prev: float32 [12288, 12288], P('row', 'col'), as said below
- energies: float32 [12288], P('row'), may hold values from 0.3 to 2
Outputs:
- casida: float32 [12288, 12288], P('row', 'col')
- vectors: float32 [12288, 8], P('row')
- images: float32 [12288, 8], P('row')
- tridiagonal: float32 [2, 8], replicated
Inputs may be any that keep to these rules, and one draw needn't show every extreme that they name: k_prev is exactly symmetric.
All inputs are finite; a program needn't handle non-finite values.
Results may differ from a plain program's by a relative error of at most 0.0003.
Values sent between devices are 32-bit elements; how exact they have to be, the bound alone decides.
A program may use at most 64 MiB of HBM per device.

v0:
```python
import jax
import jax.numpy as jnp
from jax import lax
from jax.sharding import Mesh
from jax.sharding import PartitionSpec as P

N = 12288
PC = 8
ROW = ("row_0", "row_1")
ROW_COL = ("row_0", "row_1", "col")


def laid_out(pieces, dim):
    pieces = jnp.moveaxis(pieces, 0, dim)
    shape = pieces.shape
    return pieces.reshape(*shape[:dim], shape[dim] * shape[dim + 1], *shape[dim + 2 :])


def sent_to_all(value, axis):
    copies = jnp.broadcast_to(value, (lax.axis_size(axis), *value.shape))
    return lax.all_to_all(copies, axis, split_axis=0, concat_axis=0, tiled=True)


def gathered_copies(value, axis, dim):
    return laid_out(sent_to_all(value, axis), dim)


def spread(value, axes, root):
    value = jnp.where(lax.axis_index(axes) == root, value, jnp.zeros_like(value))
    for axis in axes:
        value = lax.psum(value, axis)
    return value


def picked(value, axis, root):
    return lax.dynamic_index_in_dim(lax.all_gather(value, axis), root, 0, keepdims=False)


def over_copies(value, axis):
    everything = sent_to_all(value, axis)
    return jnp.sum(everything, axis=0)


def packed_total(arrays, axis):
    flat, at, outs = (jnp.concatenate([a.reshape(-1) for a in arrays]), 0, [])
    so_far = over_copies(flat, axis)
    for a in arrays:
        outs.append(so_far[at : at + a.size].reshape(a.shape))
        at += a.size
    return tuple(outs)


def shards(pair_factors, k_prev, energies):
    rows_here, cols_here = k_prev.shape
    per_col = lax.axis_size(ROW) // lax.axis_size("col")
    row_index = lax.axis_index(ROW)
    col_index = lax.axis_index("col")
    left_rows = gathered_copies(pair_factors, "col", 0)
    right_parts = []
    for offset in range(per_col):
        right_parts.append(spread(left_rows, ROW, per_col * col_index + offset))
    right_rows = jnp.concatenate(right_parts, axis=0)
    total = lax.dot_general(
        left_rows,
        right_rows,
        (((1,), (1,)), ((), ())),
        precision=lax.Precision.HIGHEST,
        preferred_element_type=jnp.float32,
    )
    global_rows = row_index * rows_here + jnp.arange(rows_here, dtype=jnp.int32)
    global_cols = col_index * cols_here + jnp.arange(cols_here, dtype=jnp.int32)
    on_diagonal = global_rows[:, None] == global_cols[None, :]
    casida = 4.0 * (k_prev + total) + jnp.where(on_diagonal, energies[:, None], 0.0)
    col_ids = jnp.arange(PC, dtype=jnp.int32)
    scale = jnp.sqrt(jnp.float32(N))
    diag_list = []
    sub_list = []
    head_ids = jnp.arange(PC + 1, dtype=jnp.int32)
    upper = jnp.zeros((rows_here, PC), jnp.float32)
    lower = jnp.zeros((rows_here, PC), jnp.float32)
    upper_head = jnp.zeros((PC + 1, PC), jnp.float32)
    lower_head = jnp.zeros((PC + 1, PC), jnp.float32)
    on_first = row_index == 0
    for column_at in range(PC):
        raw_column = picked(casida[:, column_at], "col", 0)
        column = (
            raw_column
            - jnp.dot(upper, lower_head[column_at], precision=lax.Precision.HIGHEST)
            - jnp.dot(lower, upper_head[column_at], precision=lax.Precision.HIGHEST)
        )
        below = jnp.where(global_rows > column_at, column, 0.0)
        head_part = jnp.where(on_first, column[: PC + 1], 0.0)
        sigma, head, upper_proj, lower_proj = packed_total(
            (
                jnp.sum(below * below),
                head_part,
                jnp.dot(upper.T, below, precision=lax.Precision.HIGHEST),
                jnp.dot(lower.T, below, precision=lax.Precision.HIGHEST),
            ),
            ROW,
        )
        diag_list.append(head[column_at])
        lead = head[column_at + 1]
        root = jnp.sqrt(sigma)
        alpha = jnp.where(lead >= 0, -root, root)
        length = jnp.sqrt(jnp.maximum(2.0 * (sigma + jnp.abs(lead) * root), 1.0))
        unit = (below - alpha * (global_rows == column_at + 1).astype(jnp.float32)) / length
        unit_head = (
            jnp.where(head_ids > column_at, head, 0.0)
            - alpha * (head_ids == column_at + 1).astype(jnp.float32)
        ) / length
        upper_unit = (upper_proj - alpha * upper_head[column_at + 1]) / length
        lower_unit = (lower_proj - alpha * lower_head[column_at + 1]) / length
        partial_cols = jnp.dot(unit, casida, precision=lax.Precision.HIGHEST)
        summed_cols = over_copies(partial_cols, ROW)
        owner_block = picked(summed_cols, "col", row_index // per_col)
        image = lax.dynamic_slice_in_dim(owner_block, row_index % per_col * rows_here, rows_here, 0)
        image = (
            image
            - jnp.dot(upper, lower_unit, precision=lax.Precision.HIGHEST)
            - jnp.dot(lower, upper_unit, precision=lax.Precision.HIGHEST)
        )
        image = 2.0 * image
        image_head_part = jnp.where(on_first, image[: PC + 1], 0.0)
        product, image_head = packed_total((jnp.sum(image * unit), image_head_part), ROW)
        partner = image - product * unit
        partner_head = image_head - product * unit_head
        pick = (col_ids == column_at).astype(jnp.float32)[None, :]
        upper = upper + unit[:, None] * pick
        lower = lower + partner[:, None] * pick
        upper_head = upper_head + unit_head[:, None] * pick
        lower_head = lower_head + partner_head[:, None] * pick
        sub_list.append(alpha)
    tridiagonal = jnp.stack([jnp.stack(diag_list), jnp.stack(sub_list)])
    return (casida, scale * upper, scale * lower, tridiagonal)


def solution(mesh):
    split = Mesh(mesh.devices.reshape(8, 4, mesh.shape["col"]), ("row_0", "row_1", "col"))
    in_specs = (P(ROW_COL, None), P(ROW, "col"), P(ROW))
    out_specs = (P(ROW, "col"), P(ROW, None), P(ROW, None), P())
    return jax.shard_map(
        shards, mesh=split, in_specs=in_specs, out_specs=out_specs, check_vma=False
    )
```

profile of v0, /device:TPU:1, one launch (start us, length us, event | category | flops | bytes accessed | tf_op | source)
XLA Modules:
  0.0 898.8 jit_solution(7743463168844762544)
XLA Ops:
  9.4 11.8 %all-to-all-start = ((f32[16,24,1024]{2,1,0:T(8,128)}), f32[16,24,1024]{2,1,0:T(8,128)S(1)}, u32[]{:S(2)}, u32[]{:S(2)}) async-start(f32[16,24,1024]{2,1,0:T(8,128)} %broadcast_in_dim.166), calls=%async_computation | async-start | bytes 3145728 | tf_op jit(solution)/shard_map/all_to_all | solution.py:21
  21.3 38.5 %all-to-all-done = f32[16,24,1024]{2,1,0:T(8,128)S(1)} async-done(((f32[16,24,1024]{2,1,0:T(8,128)}), f32[16,24,1024]{2,1,0:T(8,128)S(1)}, u32[]{:S(2)}, u32[]{:S(2)}) %all-to-all-start) | async-done | bytes 1572896 | tf_op jit(solution)/shard_map/all_to_all | solution.py:21
  61.8 93.9 %all-reduce.5.cloned.1.call-done = (f32[384,1024]{1,0:T(8,128)}, f32[384,1024]{1,0:T(8,128)}) async-done(((f32[384,1024]{1,0:T(8,128)}, f32[384,1024]{1,0:T(8,128)}), (f32[384,1024]{1,0:T(8,128)}, f32[384,1024]{1,0:T(8,128)})) %all-reduce.5.cloned.1.call-update) | async-done | bytes 3145744 | tf_op jit(solution)/shard_map/psum | solution.py:31
  159.1 85.0 %all-reduce.7.cloned.1.call-done = (f32[384,1024]{1,0:T(8,128)}, f32[384,1024]{1,0:T(8,128)}) async-done(((f32[384,1024]{1,0:T(8,128)}, f32[384,1024]{1,0:T(8,128)}), (f32[384,1024]{1,0:T(8,128)}, f32[384,1024]{1,0:T(8,128)})) %all-reduce.7.cloned.1.call-update) | async-done | bytes 3145744 | tf_op jit(solution)/shard_map/psum | solution.py:31
  244.1 7.3 fusion.13
  251.4 18.8 %all-gather = f32[6144,1]{0,1:T(1,128)S(1)} all-gather(f32[384,1]{0,1:T(1,128)S(1)} %get-tuple-element.93), channel_id=2, replica_groups=mesh['row_0'=8,'row_1'=4,'col'=16] {'col'}, dimensions={0}, use_global_device_ids=true | all-gather | bytes 26112 | tf_op jit(solution)/shard_map/all_gather | solution.py:36
  272.4 7.8 all-to-all-start.1
  280.3 8.5 all-to-all-done.1
  297.7 16.2 %all-gather.1 = f32[6144,1]{0,1:T(1,128)S(1)} all-gather(f32[384,1]{0,1:T(1,128)S(1)} %get-tuple-element.92), channel_id=3, replica_groups=mesh['row_0'=8,'row_1'=4,'col'=16] {'col'}, dimensions={0}, use_global_device_ids=true | all-gather | bytes 26112 | tf_op jit(solution)/shard_map/all_gather | solution.py:36
  316.1 15.7 %all-gather.16 = f32[16,1,768]{2,1,0:T(1,128)S(1)} all-gather(f32[1,1,768]{2,1,0:T(1,128)S(1)} %reshape.407), channel_id=4, replica_groups=mesh['row_0'=8,'row_1'=4,'col'=16] {'col'}, dimensions={0}, use_global_device_ids=true | all-gather | bytes 52224 | tf_op jit(solution)/shard_map/all_gather | solution.py:36
  333.8 9.5 %all-to-all-start.3 = ((f32[32,1,10]{2,1,0:T(1,128)}), f32[32,1,10]{2,1,0:T(1,128)S(1)}, u32[]{:S(2)}, u32[]{:S(2)}) async-start(f32[32,1,10]{2,1,0:T(1,128)} %broadcast_in_dim.173), calls=%async_computation.3 | async-start | bytes 32768 | tf_op jit(solution)/shard_map/all_to_all | solution.py:21
  343.3 8.5 all-to-all-done.3
  358.8 16.2 %all-gather.3 = f32[6144,1]{0,1:T(1,128)S(1)} all-gather(f32[384,1]{0,1:T(1,128)S(1)} %get-tuple-element.91), channel_id=5, replica_groups=mesh['row_0'=8,'row_1'=4,'col'=16] {'col'}, dimensions={0}, use_global_device_ids=true | all-gather | bytes 26112 | tf_op jit(solution)/shard_map/all_gather | solution.py:36
  380.1 9.7 %all-to-all-start.5 = ((f32[32,1,768]{2,1,0:T(1,128)}), f32[32,1,768]{2,1,0:T(1,128)S(1)}, u32[]{:S(2)}, u32[]{:S(2)}) async-start(f32[32,1,768]{2,1,0:T(1,128)} %broadcast_in_dim.175), calls=%async_computation.5 | async-start | bytes 196608 | tf_op jit(solution)/shard_map/all_to_all | solution.py:21
  390.3 8.6 all-to-all-done.5
  399.0 17.2 %all-gather.17 = f32[16,1,768]{2,1,0:T(1,128)S(1)} all-gather(f32[1,1,768]{2,1,0:T(1,128)S(1)} %reshape.409), channel_id=6, replica_groups=mesh['row_0'=8,'row_1'=4,'col'=16] {'col'}, dimensions={0}, use_global_device_ids=true | all-gather | bytes 52224 | tf_op jit(solution)/shard_map/all_gather | solution.py:36
  422.1 8.5 all-to-all-done.6
  437.7 15.9 %all-gather.5 = f32[6144,1]{0,1:T(1,128)S(1)} all-gather(f32[384,1]{0,1:T(1,128)S(1)} %get-tuple-element.90), channel_id=7, replica_groups=mesh['row_0'=8,'row_1'=4,'col'=16] {'col'}, dimensions={0}, use_global_device_ids=true | all-gather | bytes 26112 | tf_op jit(solution)/shard_map/all_gather | solution.py:36
  458.9 9.5 %all-to-all-start.8 = ((f32[32,1,768]{2,1,0:T(1,128)}), f32[32,1,768]{2,1,0:T(1,128)S(1)}, u32[]{:S(2)}, u32[]{:S(2)}) async-start(f32[32,1,768]{2,1,0:T(1,128)} %broadcast_in_dim.178), calls=%async_computation.8 | async-start | bytes 196608 | tf_op jit(solution)/shard_map/all_to_all | solution.py:21
  468.8 8.6 all-to-all-done.8
  477.5 17.2 %all-gather.18 = f32[16,1,768]{2,1,0:T(1,128)S(1)} all-gather(f32[1,1,768]{2,1,0:T(1,128)S(1)} %reshape.411), channel_id=8, replica_groups=mesh['row_0'=8,'row_1'=4,'col'=16] {'col'}, dimensions={0}, use_global_device_ids=true | all-gather | bytes 52224 | tf_op jit(solution)/shard_map/all_gather | solution.py:36
  500.7 8.5 all-to-all-done.9
  516.2 15.9 %all-gather.7 = f32[6144,1]{0,1:T(1,128)S(1)} all-gather(f32[384,1]{0,1:T(1,128)S(1)} %get-tuple-element.89), channel_id=9, replica_groups=mesh['row_0'=8,'row_1'=4,'col'=16] {'col'}, dimensions={0}, use_global_device_ids=true | all-gather | bytes 26112 | tf_op jit(solution)/shard_map/all_gather | solution.py:36
  537.4 9.5 %all-to-all-start.11 = ((f32[32,1,768]{2,1,0:T(1,128)}), f32[32,1,768]{2,1,0:T(1,128)S(1)}, u32[]{:S(2)}, u32[]{:S(2)}) async-start(f32[32,1,768]{2,1,0:T(1,128)} %broadcast_in_dim.181), calls=%async_computation.11 | async-start | bytes 196608 | tf_op jit(solution)/shard_map/all_to_all | solution.py:21
  547.4 8.6 all-to-all-done.11
  556.1 17.2 %all-gather.19 = f32[16,1,768]{2,1,0:T(1,128)S(1)} all-gather(f32[1,1,768]{2,1,0:T(1,128)S(1)} %reshape.413), channel_id=10, replica_groups=mesh['row_0'=8,'row_1'=4,'col'=16] {'col'}, dimensions={0}, use_global_device_ids=true | all-gather | bytes 52224 | tf_op jit(solution)/shard_map/all_gather | solution.py:36
  579.2 8.5 all-to-all-done.12
  594.8 15.9 %all-gather.9 = f32[6144,1]{0,1:T(1,128)S(1)} all-gather(f32[384,1]{0,1:T(1,128)S(1)} %get-tuple-element.88), channel_id=11, replica_groups=mesh['row_0'=8,'row_1'=4,'col'=16] {'col'}, dimensions={0}, use_global_device_ids=true | all-gather | bytes 26112 | tf_op jit(solution)/shard_map/all_gather | solution.py:36
  615.9 9.5 %all-to-all-start.14 = ((f32[32,1,768]{2,1,0:T(1,128)}), f32[32,1,768]{2,1,0:T(1,128)S(1)}, u32[]{:S(2)}, u32[]{:S(2)}) async-start(f32[32,1,768]{2,1,0:T(1,128)} %broadcast_in_dim.184), calls=%async_computation.14 | async-start | bytes 196608 | tf_op jit(solution)/shard_map/all_to_all | solution.py:21
  625.8 8.6 all-to-all-done.14
  634.5 17.2 %all-gather.20 = f32[16,1,768]{2,1,0:T(1,128)S(1)} all-gather(f32[1,1,768]{2,1,0:T(1,128)S(1)} %reshape.415), channel_id=12, replica_groups=mesh['row_0'=8,'row_1'=4,'col'=16] {'col'}, dimensions={0}, use_global_device_ids=true | all-gather | bytes 52224 | tf_op jit(solution)/shard_map/all_gather | solution.py:36
  657.7 8.5 all-to-all-done.15
  669.4 4.0 all-to-all-start.16
  673.4 15.9 %all-gather.11 = f32[6144,1]{0,1:T(1,128)S(1)} all-gather(f32[384,1]{0,1:T(1,128)S(1)} %get-tuple-element.87), channel_id=13, replica_groups=mesh['row_0'=8,'row_1'=4,'col'=16] {'col'}, dimensions={0}, use_global_device_ids=true | all-gather | bytes 26112 | tf_op jit(solution)/shard_map/all_gather | solution.py:36
  694.5 9.5 %all-to-all-start.17 = ((f32[32,1,768]{2,1,0:T(1,128)}), f32[32,1,768]{2,1,0:T(1,128)S(1)}, u32[]{:S(2)}, u32[]{:S(2)}) async-start(f32[32,1,768]{2,1,0:T(1,128)} %broadcast_in_dim.187), calls=%async_computation.17 | async-start | bytes 196608 | tf_op jit(solution)/shard_map/all_to_all | solution.py:21
  704.5 8.6 all-to-all-done.17
  713.2 17.2 %all-gather.21 = f32[16,1,768]{2,1,0:T(1,128)S(1)} all-gather(f32[1,1,768]{2,1,0:T(1,128)S(1)} %reshape.417), channel_id=14, replica_groups=mesh['row_0'=8,'row_1'=4,'col'=16] {'col'}, dimensions={0}, use_global_device_ids=true | all-gather | bytes 52224 | tf_op jit(solution)/shard_map/all_gather | solution.py:36
  736.3 8.5 all-to-all-done.18
  751.9 15.9 %all-gather.13 = f32[6144,1]{0,1:T(1,128)S(1)} all-gather(f32[384,1]{0,1:T(1,128)S(1)} %get-tuple-element.86), channel_id=15, replica_groups=mesh['row_0'=8,'row_1'=4,'col'=16] {'col'}, dimensions={0}, use_global_device_ids=true | all-gather | bytes 26112 | tf_op jit(solution)/shard_map/all_gather | solution.py:36
  773.0 9.5 %all-to-all-start.20 = ((f32[32,1,768]{2,1,0:T(1,128)}), f32[32,1,768]{2,1,0:T(1,128)S(1)}, u32[]{:S(2)}, u32[]{:S(2)}) async-start(f32[32,1,768]{2,1,0:T(1,128)} %broadcast_in_dim.190), calls=%async_computation.20 | async-start | bytes 196608 | tf_op jit(solution)/shard_map/all_to_all | solution.py:21
  782.9 8.6 all-to-all-done.20
  791.6 17.2 %all-gather.22 = f32[16,1,768]{2,1,0:T(1,128)S(1)} all-gather(f32[1,1,768]{2,1,0:T(1,128)S(1)} %reshape.419), channel_id=16, replica_groups=mesh['row_0'=8,'row_1'=4,'col'=16] {'col'}, dimensions={0}, use_global_device_ids=true | all-gather | bytes 52224 | tf_op jit(solution)/shard_map/all_gather | solution.py:36
  814.8 8.5 all-to-all-done.21
  831.8 7.2 all-to-all-done.22
  848.3 4.9 stack.39
  857.5 18.1 %all-gather.23 = f32[16,1,768]{2,1,0:T(1,128)S(1)} all-gather(f32[1,1,768]{2,1,0:T(1,128)S(1)} %reshape.421), channel_id=17, replica_groups=mesh['row_0'=8,'row_1'=4,'col'=16] {'col'}, dimensions={0}, use_global_device_ids=true | all-gather | bytes 52224 | tf_op jit(solution)/shard_map/all_gather | solution.py:36
  877.7 4.9 all-to-all-start.24
  883.1 8.1 all-to-all-done.24
  (279 shorter events, 134.6 us)
Async XLA Ops:
  9.4 50.3 %all-to-all-start = ((f32[16,24,1024]{2,1,0:T(8,128)}), f32[16,24,1024]{2,1,0:T(8,128)S(1)}, u32[]{:S(2)}, u32[]{:S(2)}) async-start(f32[16,24,1024]{2,1,0:T(8,128)} %broadcast_in_dim.166), calls=%async_computation | async-start | bytes 3145728 | tf_op jit(solution)/shard_map/all_to_all | solution.py:21
  21.2 134.5 %all-reduce.5.cloned.1.call-start = ((), (), s32[]{:S(2)}) async-start(), calls=%async_computation.25 | async-start | bytes 6291456 | tf_op jit(solution)/shard_map/psum | solution.py:31
  61.8 182.4 %all-reduce.7.cloned.1.call-start = ((), (), s32[]{:S(2)}) async-start(), calls=%async_computation.26 | async-start | bytes 6291456 | tf_op jit(solution)/shard_map/psum | solution.py:31
  155.7 1.3 copy-start
  157.0 87.1 %copy-start.1 = (f32[384]{0:T(512)S(1)}, f32[384]{0:T(512)}, u32[]{:S(2)}) copy-start(f32[384]{0:T(512)} %param.5) | copy-start | bytes 4612
  272.4 16.4 %all-to-all-start.1 = ((f32[32,1,26]{2,1,0:T(1,128)}), f32[32,1,26]{2,1,0:T(1,128)S(1)}, u32[]{:S(2)}, u32[]{:S(2)}) async-start(f32[32,1,26]{2,1,0:T(1,128)} %broadcast_in_dim.171), calls=%async_computation.1 | async-start | bytes 32768 | tf_op jit(solution)/shard_map/all_to_all | solution.py:21
  293.9 22.2 %all-to-all-start.2 = ((f32[32,1,768]{2,1,0:T(1,128)}), f32[32,1,768]{2,1,0:T(1,128)S(1)}, u32[]{:S(2)}, u32[]{:S(2)}) async-start(f32[32,1,768]{2,1,0:T(1,128)} %broadcast_in_dim.172), calls=%async_computation.2 | async-start | bytes 196608 | tf_op jit(solution)/shard_map/all_to_all | solution.py:21
  333.8 18.0 %all-to-all-start.3 = ((f32[32,1,10]{2,1,0:T(1,128)}), f32[32,1,10]{2,1,0:T(1,128)S(1)}, u32[]{:S(2)}, u32[]{:S(2)}) async-start(f32[32,1,10]{2,1,0:T(1,128)} %broadcast_in_dim.173), calls=%async_computation.3 | async-start | bytes 32768 | tf_op jit(solution)/shard_map/all_to_all | solution.py:21
  355.0 20.1 %all-to-all-start.4 = ((f32[32,1,26]{2,1,0:T(1,128)}), f32[32,1,26]{2,1,0:T(1,128)S(1)}, u32[]{:S(2)}, u32[]{:S(2)}) async-start(f32[32,1,26]{2,1,0:T(1,128)} %broadcast_in_dim.174), calls=%async_computation.4 | async-start | bytes 32768 | tf_op jit(solution)/shard_map/all_to_all | solution.py:21
  380.1 18.8 %all-to-all-start.5 = ((f32[32,1,768]{2,1,0:T(1,128)}), f32[32,1,768]{2,1,0:T(1,128)S(1)}, u32[]{:S(2)}, u32[]{:S(2)}) async-start(f32[32,1,768]{2,1,0:T(1,128)} %broadcast_in_dim.175), calls=%async_computation.5 | async-start | bytes 196608 | tf_op jit(solution)/shard_map/all_to_all | solution.py:21
  418.3 12.4 %all-to-all-start.6 = ((f32[32,1,10]{2,1,0:T(1,128)}), f32[32,1,10]{2,1,0:T(1,128)S(1)}, u32[]{:S(2)}, u32[]{:S(2)}) async-start(f32[32,1,10]{2,1,0:T(1,128)} %broadcast_in_dim.176), calls=%async_computation.6 | async-start | bytes 32768 | tf_op jit(solution)/shard_map/all_to_all | solution.py:21
  433.8 19.8 %all-to-all-start.7 = ((f32[32,1,26]{2,1,0:T(1,128)}), f32[32,1,26]{2,1,0:T(1,128)S(1)}, u32[]{:S(2)}, u32[]{:S(2)}) async-start(f32[32,1,26]{2,1,0:T(1,128)} %broadcast_in_dim.177), calls=%async_computation.7 | async-start | bytes 32768 | tf_op jit(solution)/shard_map/all_to_all | solution.py:21
  458.9 18.6 %all-to-all-start.8 = ((f32[32,1,768]{2,1,0:T(1,128)}), f32[32,1,768]{2,1,0:T(1,128)S(1)}, u32[]{:S(2)}, u32[]{:S(2)}) async-start(f32[32,1,768]{2,1,0:T(1,128)} %broadcast_in_dim.178), calls=%async_computation.8 | async-start | bytes 196608 | tf_op jit(solution)/shard_map/all_to_all | solution.py:21
  496.8 12.4 %all-to-all-start.9 = ((f32[32,1,10]{2,1,0:T(1,128)}), f32[32,1,10]{2,1,0:T(1,128)S(1)}, u32[]{:S(2)}, u32[]{:S(2)}) async-start(f32[32,1,10]{2,1,0:T(1,128)} %broadcast_in_dim.179), calls=%async_computation.9 | async-start | bytes 32768 | tf_op jit(solution)/shard_map/all_to_all | solution.py:21
  512.4 19.8 %all-to-all-start.10 = ((f32[32,1,26]{2,1,0:T(1,128)}), f32[32,1,26]{2,1,0:T(1,128)S(1)}, u32[]{:S(2)}, u32[]{:S(2)}) async-start(f32[32,1,26]{2,1,0:T(1,128)} %broadcast_in_dim.180), calls=%async_computation.10 | async-start | bytes 32768 | tf_op jit(solution)/shard_map/all_to_all | solution.py:21
  537.4 18.6 %all-to-all-start.11 = ((f32[32,1,768]{2,1,0:T(1,128)}), f32[32,1,768]{2,1,0:T(1,128)S(1)}, u32[]{:S(2)}, u32[]{:S(2)}) async-start(f32[32,1,768]{2,1,0:T(1,128)} %broadcast_in_dim.181), calls=%async_computation.11 | async-start | bytes 196608 | tf_op jit(solution)/shard_map/all_to_all | solution.py:21
  575.4 12.4 %all-to-all-start.12 = ((f32[32,1,10]{2,1,0:T(1,128)}), f32[32,1,10]{2,1,0:T(1,128)S(1)}, u32[]{:S(2)}, u32[]{:S(2)}) async-start(f32[32,1,10]{2,1,0:T(1,128)} %broadcast_in_dim.182), calls=%async_computation.12 | async-start | bytes 32768 | tf_op jit(solution)/shard_map/all_to_all | solution.py:21
  590.9 19.8 %all-to-all-start.13 = ((f32[32,1,26]{2,1,0:T(1,128)}), f32[32,1,26]{2,1,0:T(1,128)S(1)}, u32[]{:S(2)}, u32[]{:S(2)}) async-start(f32[32,1,26]{2,1,0:T(1,128)} %broadcast_in_dim.183), calls=%async_computation.13 | async-start | bytes 32768 | tf_op jit(solution)/shard_map/all_to_all | solution.py:21
  615.9 18.6 %all-to-all-start.14 = ((f32[32,1,768]{2,1,0:T(1,128)}), f32[32,1,768]{2,1,0:T(1,128)S(1)}, u32[]{:S(2)}, u32[]{:S(2)}) async-start(f32[32,1,768]{2,1,0:T(1,128)} %broadcast_in_dim.184), calls=%async_computation.14 | async-start | bytes 196608 | tf_op jit(solution)/shard_map/all_to_all | solution.py:21
  653.8 12.4 %all-to-all-start.15 = ((f32[32,1,10]{2,1,0:T(1,128)}), f32[32,1,10]{2,1,0:T(1,128)S(1)}, u32[]{:S(2)}, u32[]{:S(2)}) async-start(f32[32,1,10]{2,1,0:T(1,128)} %broadcast_in_dim.185), calls=%async_computation.15 | async-start | bytes 32768 | tf_op jit(solution)/shard_map/all_to_all | solution.py:21
  669.4 20.0 %all-to-all-start.16 = ((f32[32,1,26]{2,1,0:T(1,128)}), f32[32,1,26]{2,1,0:T(1,128)S(1)}, u32[]{:S(2)}, u32[]{:S(2)}) async-start(f32[32,1,26]{2,1,0:T(1,128)} %broadcast_in_dim.186), calls=%async_computation.16 | async-start | bytes 32768 | tf_op jit(solution)/shard_map/all_to_all | solution.py:21
  694.5 18.6 %all-to-all-start.17 = ((f32[32,1,768]{2,1,0:T(1,128)}), f32[32,1,768]{2,1,0:T(1,128)S(1)}, u32[]{:S(2)}, u32[]{:S(2)}) async-start(f32[32,1,768]{2,1,0:T(1,128)} %broadcast_in_dim.187), calls=%async_computation.17 | async-start | bytes 196608 | tf_op jit(solution)/shard_map/all_to_all | solution.py:21
  732.4 12.4 %all-to-all-start.18 = ((f32[32,1,10]{2,1,0:T(1,128)}), f32[32,1,10]{2,1,0:T(1,128)S(1)}, u32[]{:S(2)}, u32[]{:S(2)}) async-start(f32[32,1,10]{2,1,0:T(1,128)} %broadcast_in_dim.188), calls=%async_computation.18 | async-start | bytes 32768 | tf_op jit(solution)/shard_map/all_to_all | solution.py:21
  748.0 19.8 %all-to-all-start.19 = ((f32[32,1,26]{2,1,0:T(1,128)}), f32[32,1,26]{2,1,0:T(1,128)S(1)}, u32[]{:S(2)}, u32[]{:S(2)}) async-start(f32[32,1,26]{2,1,0:T(1,128)} %broadcast_in_dim.189), calls=%async_computation.19 | async-start | bytes 32768 | tf_op jit(solution)/shard_map/all_to_all | solution.py:21
  773.0 18.6 %all-to-all-start.20 = ((f32[32,1,768]{2,1,0:T(1,128)}), f32[32,1,768]{2,1,0:T(1,128)S(1)}, u32[]{:S(2)}, u32[]{:S(2)}) async-start(f32[32,1,768]{2,1,0:T(1,128)} %broadcast_in_dim.190), calls=%async_computation.20 | async-start | bytes 196608 | tf_op jit(solution)/shard_map/all_to_all | solution.py:21
  810.9 12.4 %all-to-all-start.21 = ((f32[32,1,10]{2,1,0:T(1,128)}), f32[32,1,10]{2,1,0:T(1,128)S(1)}, u32[]{:S(2)}, u32[]{:S(2)}) async-start(f32[32,1,10]{2,1,0:T(1,128)} %broadcast_in_dim.191), calls=%async_computation.21 | async-start | bytes 32768 | tf_op jit(solution)/shard_map/all_to_all | solution.py:21
  826.6 12.5 %all-to-all-start.22 = ((f32[32,1,26]{2,1,0:T(1,128)}), f32[32,1,26]{2,1,0:T(1,128)S(1)}, u32[]{:S(2)}, u32[]{:S(2)}) async-start(f32[32,1,26]{2,1,0:T(1,128)} %broadcast_in_dim.192), calls=%async_computation.22 | async-start | bytes 32768 | tf_op jit(solution)/shard_map/all_to_all | solution.py:21
  844.4 13.0 %all-to-all-start.23 = ((f32[32,1,768]{2,1,0:T(1,128)}), f32[32,1,768]{2,1,0:T(1,128)S(1)}, u32[]{:S(2)}, u32[]{:S(2)}) async-start(f32[32,1,768]{2,1,0:T(1,128)} %broadcast_in_dim.193), calls=%async_computation.23 | async-start | bytes 196608 | tf_op jit(solution)/shard_map/all_to_all | solution.py:21
  877.7 13.5 %all-to-all-start.24 = ((f32[32,1,10]{2,1,0:T(1,128)}), f32[32,1,10]{2,1,0:T(1,128)S(1)}, u32[]{:S(2)}, u32[]{:S(2)}) async-start(f32[32,1,10]{2,1,0:T(1,128)} %broadcast_in_dim.194), calls=%async_computation.24 | async-start | bytes 32768 | tf_op jit(solution)/shard_map/all_to_all | solution.py:21
Sparse Core Ops, SparseCore 0:
  61.9 93.7 all-reduce.4
  158.1 85.9 all-reduce.6
where the time goes:
time: 901 us; the launch traced here: 899 us
  waiting for transfers between devices  356 us (40%)
  blocking collectives  268 us (30%)
  starting transfers between devices  149 us (17%)
  between operations  36.2 us (4%)
  local copies, waits for them, and re-layouts  33.9 us (4%)
  other arithmetic  30.2 us (3%)
  matrix products  25.4 us (3%)
    all_gather x16, blocking collectives, picked(): lax.all_gather(value, axis)  268 us
    psum x2, waiting for transfers between devices, spread(): value = lax.psum(value, axis)  179 us
    all_to_all x25, waiting for transfers between devices, sent_to_all(): return lax.all_to_all(copies, axis, split_axis=0, concat_axis=0, tiled=True)  177 us
    all_to_all x25, starting transfers between devices, sent_to_all(): return lax.all_to_all(copies, axis, split_axis=0, concat_axis=0, tiled=True)  149 us
  transfers between devices with their start and end apart: 27, of which 20 were waited for; matrix products, arithmetic and copies ran while one was open for 2% of the time, Pallas kernels for 0%

commit v1 on v0

v1 whole, which is shorter than its diff:
```python
import functools

import jax
import jax.numpy as jnp
from jax import lax
from jax.experimental import pallas as pl
from jax.experimental.pallas import tpu as pltpu
from jax.sharding import PartitionSpec as P

N = 12288
PC = 8
AUX = 1024
CH = 24
ROWS = 384
COLS = 768
MESH = pl.DeviceIdType.MESH
HI = lax.Precision.HIGHEST


def chunk(slot):
    return pl.ds(pl.multiple_of(slot * CH, 8), CH)


def remote(src, dst, send, recv, row, col):
    return pltpu.make_async_remote_copy(
        src_ref=src, dst_ref=dst, send_sem=send, recv_sem=recv,
        device_id=(row, col), device_id_type=MESH,
    )


def iota(shape, axis):
    return lax.broadcasted_iota(jnp.int32, shape, axis)


def lane_sum(a):
    width = a.shape[1] // 128
    total = a[:, 0:128]
    for t in range(1, width):
        total = total + a[:, 128 * t : 128 * (t + 1)]
    return total


def kernel(
    pf, kp_hbm, en, casida, uw, tri,
    left, right, kp, a, ae, v, zbuf, xbuf, tbuf, abuf, spare,
    local, ls, lr, rs, rr, zs, zr, xs, xr, ts, tr, bs, br,
):
    r = lax.axis_index("row")
    c = lax.axis_index("col")
    y, x = r // 4, r % 4
    z, k = c // 2, c % 2

    kp_in = pltpu.make_async_copy(kp_hbm, kp, local.at[0])
    kp_in.start()
    own_in = pltpu.make_async_copy(pf, left.at[chunk(c)], local.at[1])
    own_in.start()

    barrier = pltpu.get_barrier_semaphore()

    def greet_row(d, _):
        pl.semaphore_signal(barrier, inc=1, device_id=((r + d) % 32, c), device_id_type=MESH)
        return 0

    def greet_col(d, _):
        pl.semaphore_signal(barrier, inc=1, device_id=(r, (c + d) % 16), device_id_type=MESH)
        return 0

    lax.fori_loop(1, 32, greet_row, 0)
    lax.fori_loop(1, 16, greet_col, 0)
    v[...] = jnp.zeros_like(v)
    pl.semaphore_wait(barrier, 46)
    own_in.wait()

    def l_copy(slot, direction):
        if direction == 0:
            col = (z + 1) % 8 * 2 + k
        elif direction == 1:
            col = (z + 7) % 8 * 2 + k
        else:
            col = 2 * z + (1 - k)
        return remote(left.at[chunk(slot)], left.at[chunk(slot)], ls.at[direction, slot], lr.at[slot], r, col)

    def l_wait(slot):
        pltpu.make_async_copy(left.at[chunk(slot)], left.at[chunk(slot)], lr.at[slot]).wait()

    def stage_slots(i, core):
        return (z + 8 - i) % 8 * 2 + core, (z + i) % 8 * 2 + core

    def r_rows(b, slot):
        return pl.ds(pl.multiple_of(b * ROWS + slot * CH, 8), CH)

    def r_copy(b, slot, direction, from_left):
        row = (
            (y + 1) % 8 * 4 + x,
            (y + 7) % 8 * 4 + x,
            y * 4 + (x + 1) % 4,
            y * 4 + (x + 3) % 4,
        )[direction]
        src = left.at[chunk(slot)] if from_left else right.at[r_rows(b, slot)]
        return remote(src, right.at[r_rows(b, slot)], rs.at[direction, b, slot], rr.at[b, slot], row, c)

    dy = (y - z + 8) % 8
    ydist = jnp.where(dy <= 4, dy, 8 - dy)
    groups = []
    for b in range(2):
        dx = (x - (2 * k + b) + 4) % 4
        xdist = jnp.where(dx <= 2, dx, 1)
        groups.append((b, dx, ydist + xdist))

    def r_roles(b, dx, slot, even):
        at_source = (dx == 0) & (dy == 0)
        column = dx == 0
        yield 0, True, at_source
        yield 1, True, at_source
        yield 0, False, column & (dy >= 1) & (dy <= 3)
        yield 1, False, column & (dy >= 6)
        yield 2, True, at_source
        yield 3, True, at_source
        yield 2, False, (column & (dy > 0)) | ((dx == 1) & even)
        yield 3, False, (column & (dy > 0)) | ((dx == 3) & (not even))

    def local_copy(b, slot):
        return pltpu.make_async_copy(left.at[chunk(slot)], right.at[r_rows(b, slot)], rr.at[b, slot])

    def r_process(b, dx, slot, even):
        at_source = (dx == 0) & (dy == 0)

        @pl.when(at_source)
        def _():
            local_copy(b, slot).start()

        @pl.when(jnp.logical_not(at_source))
        def _():
            pltpu.make_async_copy(right.at[r_rows(b, slot)], right.at[r_rows(b, slot)], rr.at[b, slot]).wait()

        for direction, from_left, cond in r_roles(b, dx, slot, even):
            @pl.when(cond)
            def _(direction=direction, from_left=from_left):
                r_copy(b, slot, direction, from_left).start()

    def r_stage(t, core_same):
        core = k if core_same else 1 - k
        for b, dx, dist in groups:
            i = t - dist
            @pl.when((i >= 0) & (i <= 4))
            def _(b=b, dx=dx, i=i):
                minus, plus = stage_slots(i, core)
                r_process(b, dx, minus, core_same)
                @pl.when((i >= 1) & (i <= 3))
                def _():
                    r_process(b, dx, plus, core_same)

    def gather_step(t, _):
        @pl.when(t == 0)
        def _():
            for direction in range(3):
                l_copy(c, direction).start()

        @pl.when((t >= 1) & (t <= 4))
        def _():
            minus, plus = stage_slots(t, k)
            l_wait(minus)
            @pl.when(t < 4)
            def _():
                l_copy(minus, 0).start()
            l_copy(minus, 2).start()
            @pl.when(t < 4)
            def _():
                l_wait(plus)
                @pl.when(t < 3)
                def _():
                    l_copy(plus, 1).start()
                l_copy(plus, 2).start()

        r_stage(t, True)

        @pl.when(t <= 4)
        def _():
            minus, plus = stage_slots(t, 1 - k)
            l_wait(minus)
            @pl.when((t >= 1) & (t <= 3))
            def _():
                l_wait(plus)

        r_stage(t, False)
        return 0

    lax.fori_loop(0, 11, gather_step, 0)

    def l_drain(slot, _):
        dz = (slot // 2 - z + 8) % 8
        mine = slot % 2 == k
        @pl.when(mine & ((dz == 0) | (dz >= 5)))
        def _():
            l_copy(slot, 0).wait_send()
        @pl.when(mine & (dz <= 2))
        def _():
            l_copy(slot, 1).wait_send()
        @pl.when(mine)
        def _():
            l_copy(slot, 2).wait_send()
        for b, dx, _d in groups:
            at_source = (dx == 0) & (dy == 0)
            @pl.when(at_source)
            def _(b=b):
                local_copy(b, slot).wait()
            for same in (True, False):
                @pl.when(mine if same else jnp.logical_not(mine))
                def _(b=b, dx=dx, same=same):
                    for direction, from_left, cond in r_roles(b, dx, slot, same):
                        @pl.when(cond)
                        def _(direction=direction, from_left=from_left):
                            r_copy(b, slot, direction, from_left).wait_send()
        return 0

    lax.fori_loop(0, 16, l_drain, 0)
    kp_in.wait()

    def block(t, _):
        at = pl.ds(pl.multiple_of(t * 128, 128), 128)
        prod = lax.dot_general(
            left[...], right[at, :], (((1,), (1,)), ((), ())),
            precision=HI, preferred_element_type=jnp.float32,
        )
        a[:, at] = 4.0 * (kp[:, at] + prod)
        return 0

    lax.fori_loop(0, 6, block, 0)
    eye = iota((ROWS, ROWS), 0) == iota((ROWS, ROWS), 1)
    for b in range(2):
        @pl.when(r == 2 * c + b)
        def _(b=b):
            at = slice(b * ROWS, (b + 1) * ROWS)
            a[:, at] = a[:, at] + jnp.where(eye, en[...], 0.0)
    out = pltpu.make_async_copy(a, casida, local.at[0])
    out.start()

    def peers_row(send):
        def body(d, _):
            send((r + d) % 32, c)
            return 0
        lax.fori_loop(1, 32, body, 0)

    def peers_col(send):
        def body(d, _):
            send(r, (c + d) % 16)
            return 0
        lax.fori_loop(1, 16, body, 0)

    def ae_copy(row, col):
        return remote(ae, ae, bs.at[0], br.at[0], row, col)

    def a0_copy(row, col):
        return remote(abuf, abuf, bs.at[1], br.at[1], row, col)

    @pl.when(c == 0)
    def _():
        head = a[:, 0:128].T
        for i in range(PC + 1):
            ae[i] = head[i : i + 1, :]
        peers_col(lambda row, col: ae_copy(row, col).start())

    @pl.when(r == 0)
    def _():
        abuf[...] = a[0:1, :]
        peers_row(lambda row, col: a0_copy(row, col).start())

    @pl.when(c != 0)
    def _():
        ae_copy(r, c).wait_recv()

    @pl.when(r != 0)
    def _():
        a0_copy(r, c).wait_recv()

    lane = iota((1, 128), 1)
    row_ids = r * ROWS + iota((1, ROWS), 1)
    col_ids = c * COLS + iota((1, COLS), 1)
    sub24 = iota((24, 128), 0)
    lane24 = iota((24, 128), 1)

    def column_of(row_form, shift):
        return jnp.sum(jnp.where(lane24 == sub24 + shift, row_form, 0.0), axis=1, keepdims=True)

    def zdrain(sem, ref, count):
        pltpu.make_async_copy(ref.at[pl.ds(0, count)], ref.at[pl.ds(0, count)], sem).wait()

    full_c = abuf[...]
    full_r = ae[0]
    heads = jnp.zeros((24, 128), jnp.float32)
    dots = jnp.zeros((24, 1), jnp.float32)
    diag = jnp.zeros((1, 128), jnp.float32)
    sub = jnp.zeros((1, 128), jnp.float32)
    for j in range(PC):
        xc = jnp.where(col_ids > j, full_c, 0.0)
        xrow = jnp.where(row_ids > j, full_r, 0.0)
        acc = a[:, 0:128] * xc[:, 0:128]
        for t in range(1, 6):
            acc = acc + a[:, 128 * t : 128 * (t + 1)] * xc[:, 128 * t : 128 * (t + 1)]
        part = lax.dot_general(
            jnp.ones((8, 128), jnp.float32), acc, (((1,), (1,)), ((), ())),
            precision=HI, preferred_element_type=jnp.float32,
        )[0:1, :]
        sq = lane_sum(xc * xc)
        sq = sq + pltpu.roll(sq, 64, 1)
        side = jnp.where(lane >= 64, sq, jnp.where((lane < 16) & (c == 0), full_c[:, 0:128], 0.0))
        zbuf[j, c] = jnp.concatenate([part, side], axis=1)
        peers_col(lambda row, col: remote(zbuf.at[j, c], zbuf.at[j, c], zs.at[j], zr.at[j], row, col).start())
        zdrain(zr.at[j], zbuf.at[j], 15)
        tot = zbuf[j, 0]
        for s in range(1, 16):
            tot = tot + zbuf[j, s]
        side = tot[:, ROWS:]
        head_full = jnp.where(lane < 16, side, 0.0)
        hx = jnp.where(lane > j, head_full, 0.0)
        sigma = jnp.sum(jnp.where(lane >= 64, side, 0.0), axis=1, keepdims=True)
        lead = hx[:, j + 1 : j + 2]
        root = jnp.sqrt(sigma)
        alpha = jnp.where(lead >= 0, -root, root)
        length = jnp.sqrt(jnp.maximum(2.0 * (sigma + jnp.abs(lead) * root), 1.0))
        inv = 1.0 / length
        diag = jnp.where(lane == j, head_full[:, j : j + 1], diag)
        sub = jnp.where(lane == j, alpha, sub)
        uc = (xc - jnp.where(col_ids == j + 1, alpha, 0.0)) * inv
        ur = (xrow - jnp.where(row_ids == j + 1, alpha, 0.0)) * inv
        hu = (hx - jnp.where(lane == j + 1, alpha, 0.0)) * inv
        top = hu[:, j + 1 : j + 2]
        aej = ae[j + 1]
        au = (tot[:, :ROWS] - alpha * aej) * inv
        vv = v[...]
        hcol = heads[:, j + 1 : j + 2]
        coef = (dots - alpha * hcol) * inv
        swap_coef = jnp.concatenate([coef[8:16], coef[0:8]], axis=0)
        swap_head = jnp.concatenate([hcol[8:16], hcol[0:8]], axis=0)
        p = 2.0 * (au - jnp.sum(vv[0:16] * swap_coef, axis=0, keepdims=True))
        cand = aej - jnp.sum(vv[0:16] * swap_head, axis=0, keepdims=True) - top * p
        v[j : j + 1, :] = ur
        v[16:17, :] = p
        vv = v[...]
        below = row_ids > j + 1
        sm = jnp.where(below, cand, 0.0)
        um = jnp.where(below, ur, 0.0)
        ds_ = jnp.sum(lane_sum(vv * sm), axis=1, keepdims=True)
        dm_ = jnp.sum(lane_sum(vv * um), axis=1, keepdims=True)
        row = jnp.sum(
            jnp.where(lane24 == sub24, ds_, 0.0) + jnp.where(lane24 == sub24 + 32, dm_, 0.0),
            axis=0, keepdims=True,
        )
        ph = jnp.where((lane < 16) & (r == 0), p[:, 0:128], 0.0)
        xbuf[j, r] = row + pltpu.roll(ph, 64, 1)
        peers_row(lambda row_, col: remote(xbuf.at[j, r], xbuf.at[j, r], xs.at[j], xr.at[j], row_, col).start())

        def t_copy(b, row_, col):
            return remote(tbuf.at[j, b], tbuf.at[j, b], ts.at[j], tr.at[j, b], row_, col)

        if j + 1 < PC:
            for b in range(2):
                @pl.when(r == 2 * c + b)
                def _(b=b):
                    tbuf[j, b] = cand
                    peers_row(lambda row_, col: t_copy(b, row_, col).start())
        zdrain(xr.at[j], xbuf.at[j], 31)
        sums = xbuf[j, 0]
        for s in range(1, 32):
            sums = sums + xbuf[j, s]
        hp = jnp.where(lane < 16, pltpu.roll(sums, 64, 1), 0.0)
        dsc = column_of(sums, 0)
        dmc = column_of(sums, 32)
        ptop = hp[:, j + 1 : j + 2]
        kappa = dmc[16:17] + ptop * top
        beta = 2.0 * kappa * top - ptop
        w = p - kappa * ur
        hw = hp - kappa * hu
        v[8 + j : 9 + j, :] = w
        heads = jnp.where(sub24 == j, hu, jnp.where(sub24 == 8 + j, hw, heads))
        if j + 1 < PC:
            for b in range(2):
                @pl.when(r != 2 * c + b)
                def _(b=b):
                    t_copy(b, r, c).wait_recv()
            full_c = jnp.concatenate([tbuf[j, 0], tbuf[j, 1]], axis=1) + beta * uc
            full_r = cand + beta * ur
            dots = dsc + beta * dmc
            wdot = dots[16:17] - kappa * dots[j : j + 1]
            dots = jnp.where(iota((24, 1), 0) == 8 + j, wdot, dots)

    uw[...] = v[0:16, :]
    tri[...] = jnp.concatenate([diag, sub], axis=0)

    for j in range(PC):
        zdrain(zs.at[j], zbuf.at[j], 15)
        zdrain(xs.at[j], xbuf.at[j], 31)
        if j + 1 < PC:
            @pl.when(r // 2 == c)
            def _(j=j):
                zdrain(ts.at[j], spare, 31)

    @pl.when(c == 0)
    def _():
        zdrain(bs.at[0], spare, 15 * (PC + 1))

    @pl.when(r == 0)
    def _():
        zdrain(bs.at[1], spare, 31 * 2)

    out.wait()


def solution(mesh):
    f32 = jnp.float32
    vmem = pl.BlockSpec(memory_space=pltpu.VMEM)
    hbm = pl.BlockSpec(memory_space=pl.ANY)
    dma = pltpu.SemaphoreType.DMA

    def shards(pair_factors, k_prev, energies):
        casida, uw, tri = pl.pallas_call(
            kernel,
            out_shape=(
                jax.ShapeDtypeStruct((ROWS, COLS), f32),
                jax.ShapeDtypeStruct((2 * PC, ROWS), f32),
                jax.ShapeDtypeStruct((2, 128), f32),
            ),
            in_specs=[hbm, hbm, vmem],
            out_specs=(hbm, vmem, vmem),
            scratch_shapes=[
                pltpu.VMEM((ROWS, AUX), f32),
                pltpu.VMEM((COLS, AUX), f32),
                pltpu.VMEM((ROWS, COLS), f32),
                pltpu.VMEM((ROWS, COLS), f32),
                pltpu.VMEM((PC + 1, 1, ROWS), f32),
                pltpu.VMEM((24, ROWS), f32),
                pltpu.VMEM((PC, 16, 1, ROWS + 128), f32),
                pltpu.VMEM((PC, 32, 1, 128), f32),
                pltpu.VMEM((PC, 2, 1, ROWS), f32),
                pltpu.VMEM((1, COLS), f32),
                pltpu.VMEM((15 * (PC + 1), 1, ROWS), f32),
                dma((2,)),
                dma((3, 16)), dma((16,)), dma((4, 2, 16)), dma((2, 16)),
                dma((PC,)), dma((PC,)), dma((PC,)), dma((PC,)),
                dma((PC,)), dma((PC, 2)), dma((2,)), dma((2,)),
            ],
            compiler_params=pltpu.CompilerParams(collective_id=0, has_side_effects=True),
            name="casida",
        )(pair_factors, k_prev, energies.reshape(1, ROWS))
        scale = jnp.sqrt(f32(N))
        return casida, scale * uw[:PC].T, scale * uw[PC:].T, tri[:, :PC]

    return jax.shard_map(
        shards, mesh=mesh,
        in_specs=(P(("row", "col"), None), P("row", "col"), P("row")),
        out_specs=(P("row", "col"), P("row", None), P("row", None), P()),
        check_vma=False,
    )
```

time: 901 us -> 181 us (0.20)
  waiting for transfers between devices: 356 us -> 0 us
  blocking collectives: 268 us -> 0 us
  Pallas kernels: 0 us -> 174 us
  starting transfers between devices: 149 us -> 0 us
  between operations: 36.2 us -> 0.64 us
  local copies, waits for them, and re-layouts: 33.9 us -> 4.17 us
  other arithmetic: 30.2 us -> 1.33 us
  matrix products: 25.4 us -> 0 us
    all_gather x16 -> x0, blocking collectives: 268 us -> none  [picked(): lax.all_gather(value, axis)]
    psum x2 -> x0, waiting for transfers between devices: 179 us -> none  [spread(): value = lax.psum(value, axis)]
    all_to_all x25 -> x0, waiting for transfers between devices: 177 us -> none  [sent_to_all(): return lax.all_to_all(copies, axis, split_axis=0, concat_axis=0, tiled=True)]
    pallas_call x0 -> x1, Pallas kernels: none -> 174 us  [shards(): pl.pallas_call(kernel, out_shape=(jax.ShapeDtypeStruct((ROWS, COLS), f32)...]
    all_to_all x25 -> x0, starting transfers between devices: 149 us -> none  [sent_to_all(): return lax.all_to_all(copies, axis, split_axis=0, concat_axis=0, tiled=True)]
    dot_general x52 -> x0, matrix products: 25.4 us -> none  [the longest x8 8.49 us: shards(): partial_cols = jnp.dot(unit, casida, precision=lax.Precision.HIGHEST)]
    broadcast_in_dim x25 -> x0, local copies, waits for them, and re-layouts: 17.6 us -> none  [sent_to_all(): copies = jnp.broadcast_to(value, (lax.axis_size(axis), *value.shape))]
    concatenate x16 -> x0, other arithmetic: 11.7 us -> none  [packed_total(): flat, at, outs = (jnp.concatenate([a.reshape(-1) for a in arrays]), 0, [])]
  transfers between devices with their start and end apart: 27 -> 0, of which waited for: 20 -> 0; matrix products, arithmetic and copies ran while one was open for 2% -> 0% of each run, Pallas kernels for 0% -> 0%
where the time goes in v1:
time: 181 us
  Pallas kernels  174 us (96%)
  local copies, waits for them, and re-layouts  4.17 us (2%)
    pallas_call x1, Pallas kernels, shards(): pl.pallas_call(kernel, out_shape=(jax.ShapeDtypeStruct((ROWS, COLS), f32)...  174 us

profile of v1, /device:TPU:1, one launch (start us, length us, event | category | flops | bytes accessed | tf_op | source)
XLA Modules:
  0.0 180.6 jit_solution(7817722196757921053)
XLA Ops:
  0.6 1.2 reshape.11.en
  1.9 174.5 %casida.1 = (f32[384,768]{1,0:T(8,128)}, f32[16,384]{1,0:T(8,128)}, f32[2,128]{1,0:T(2,128)}) custom-call(f32[24,1024]{1,0:T(8,128)} %pf.1, f32[384,768]{1,0:T(8,128)} %kp_hbm.1, f32[1,384]{1,0:T(1,128)} %reshape.11.en), custom_call_target="tpu_custom_call" | custom-call | tf_op jit(solution)/shard_map/casida/pallas_call | solution.py:416
  176.4 1.3 multiply_bitcast_fusion
  177.7 0.0 copy-start
  177.7 2.4 %copy.9 = f32[384,768]{1,0:T(8,128)} copy(f32[384,768]{1,0:T(8,128)} %get-tuple-element.16) | data formatting | bytes 2359296
  180.1 0.0 copy-done
  180.1 0.6 copy.10
Async XLA Ops:
  177.7 2.4 %copy-start = (f32[2,128]{1,0:T(2,128)S(1)}, f32[2,128]{1,0:T(2,128)}, u32[]{:S(2)}) copy-start(f32[2,128]{1,0:T(2,128)} %get-tuple-element.9) | copy-start | bytes 3076
